TPU v7x, 32 devices: a whole 2x2x4 slice. The times are simulated.
32 devices in a mesh: gx: 8 (over z, core), gy: 2 (over y), gz: 2 (over x).
Axes of the slice: x: 2, y: 2, z: 4, core: 2. Of those that a mesh axis runs over, the one named last changes fastest.
Arguments:
- volume: float32 [128, 128, 256], P('gx', 'gy', 'gz'), may hold values from -6 to 6
- weights: float32 [64, 8, 128], P(None, None, 'gx'), may hold values from -0.1875 to 0.1875
- offsets: int32 [64, 8], P(None, 'gx'), may hold values from 0 to 57, as said below
- measured: float32 [64, 128, 256], P('gx', 'gy', 'gz'), may hold values from -6 to 6
Outputs:
- gradient: float32 [128, 128, 256], P('gx', 'gy', 'gz')
- residual: float32 [64, 128, 256], P('gx', 'gy', 'gz')
- misfit: float32 [], replicated
Inputs may be any that keep to these rules, and one draw needn't show every extreme that they name: offsets[a, b] shifts angle a on brick b; the values 0 and 57 both occur.
All inputs are finite; a program needn't handle non-finite values.
Results may differ from a plain program's by a relative error of at most 0.0003.
Values sent between devices are 32-bit elements; how exact they have to be, the bound alone decides.
A program may use at most 64 MiB of HBM per device.

v0:
```python
import jax
import jax.numpy as jnp
from jax import lax
from jax.sharding import PartitionSpec as P


def passed_along(x, axis, by):
    count = lax.axis_size(axis)
    pairs = [(i, i + by) for i in range(count) if 0 <= i + by < count]
    return lax.ppermute(x, axis, pairs)


def body(volume, weights, offsets, measured):
    cols, rows, depth = volume.shape
    angles = weights.shape[0]
    taps = weights.shape[1]
    blocks = angles // 8
    shifts = offsets[:, 0]
    wblk = weights.reshape(blocks, 8, taps, cols)
    sblk = shifts.reshape(blocks, 8)

    def project(args):
        wb, sb = args
        spread = jnp.einsum("adc,cyz->adyz", wb, volume, precision=lax.Precision.HIGHEST)
        padded = jnp.pad(spread, ((0, 0), (0, 0), (rows, rows), (0, 0)))

        def project_per_angle(plane, shift):
            window = lax.dynamic_slice_in_dim(plane, shift, 2 * rows + taps - 1, 1)
            total = jnp.zeros((2 * rows, depth), jnp.float32)
            for tap in range(taps):
                total = total + window[tap, tap : tap + 2 * rows]
            return total

        return jax.vmap(project_per_angle)(padded, sb)

    window_rows = lax.map(project, (wblk, sblk)).reshape(angles, 2 * rows, depth)
    lower = window_rows[:, :rows]
    upper = window_rows[:, rows:]
    partial_value = upper + passed_along(lower, "gy", -1)
    summed = lax.psum_scatter(partial_value, "gx", scatter_dimension=0, tiled=True)
    resid_share = summed - measured
    before = passed_along(resid_share, "gy", 1)
    resid_all, before_all = (
        lax.all_gather(resid_share, "gx", axis=0, tiled=True),
        lax.all_gather(before, "gx", axis=0, tiled=True),
    )
    extended = jnp.concatenate([before_all, resid_all], axis=1)
    rblk = extended.reshape(blocks, 8, 2 * rows, depth)

    def backward(grad, args):
        wb, sb, rb = args

        def backward_per_angle(plane, shift):
            start = rows - shift - (taps - 1)
            window = lax.dynamic_slice_in_dim(plane, start, rows + taps - 1, 0)
            return jnp.stack(
                [window[taps - 1 - tap : taps - 1 - tap + rows] for tap in range(taps)]
            )

        sheared = jax.vmap(backward_per_angle)(rb, sb)
        grad = grad + jnp.einsum("adc,adyz->cyz", wb, sheared, precision=lax.Precision.HIGHEST)
        return (grad, None)

    gradient, unused = lax.scan(
        backward, jnp.zeros((cols, rows, depth), jnp.float32), (wblk, sblk, rblk)
    )
    entries = angles * rows * depth * lax.axis_size("gy") * lax.axis_size("gz")
    misfit = lax.psum(jnp.sum(resid_share * resid_share), ("gx", "gy", "gz")) / entries
    return (gradient, resid_share, misfit)


def solution(mesh):
    in_specs = (P("gx", "gy", "gz"), P(None, None, "gx"), P(None, "gx"), P("gx", "gy", "gz"))
    out_specs = (P("gx", "gy", "gz"), P("gx", "gy", "gz"), P())
    return jax.shard_map(body, mesh=mesh, in_specs=in_specs, out_specs=out_specs, check_vma=False)
```

profile of v0, /device:TPU:0, one launch (start us, length us, event | category | flops | bytes accessed | tf_op | source)
XLA Modules:
  0.0 486.3 jit_solution(15363461617519916820)
XLA Ops:
  12.2 215.0 %while.27 = (s32[]{:T(128)}, f32[8,8,128,128]{3,2,1,0:T(8,128)}, f32[8,8,8,16]{3,2,1,0:T(8,128)}, f32[16,64,128]{2,0,1:T(8,128)S(1)}, s32[8,8]{1,0:T(8,128)S(1)}, /*index=5*/s32[]{:T(128)}, f32[]{:T(128)}) while((s32[]{:T(128)}, f32[8,8,128,128]{3,2,1,0:T(8,128)}, f32[8,8,8,16]{3,2,1,0:T(8,128)}, f32[16,64,128]{2,0,1:T(8,128)S(1)}, ...), condition=%wide.region_1.2_spmd, body=%wide.region_0.1_spmd.sunk | while | flops 101580864 | bytes 29852948 | solution.py:36
  18.5 6.1 %gather_fusion = f32[8,8,135,128]{3,1,2,0:T(8,128)} fusion(f32[8,8,192,128]{3,1,0,2:T(8,128)} %pad.13.clone.2, s32[8]{0:T(128)S(1)} %or_bitcast_fusion.4), kind=kCustom, calls=%fused_computation.clone.1 | custom fusion | bytes 8847488 | tf_op jit(solution)/shard_map/while/body/eval_jaxpr/vmap()/gather | solution.py:28
  24.6 13.6 %slice_add_fusion.9 = f32[8,1,128,128]{3,1,2,0:T(1,128)S(1)} fusion(f32[8,8,135,128]{3,1,2,0:T(8,128)} %gather_fusion), kind=kLoop, calls=%fused_computation.2.clone.1 | loop fusion | flops 917504 | bytes 4718592 | tf_op jit(solution)/shard_map/while/body/eval_jaxpr/vmap()/add | solution.py:31
  45.4 6.1 %gather_fusion = f32[8,8,135,128]{3,1,2,0:T(8,128)} fusion(f32[8,8,192,128]{3,1,0,2:T(8,128)} %pad.13.clone.2, s32[8]{0:T(128)S(1)} %or_bitcast_fusion.4), kind=kCustom, calls=%fused_computation.clone.1 | custom fusion | bytes 8847488 | tf_op jit(solution)/shard_map/while/body/eval_jaxpr/vmap()/gather | solution.py:28
  51.5 13.6 %slice_add_fusion.9 = f32[8,1,128,128]{3,1,2,0:T(1,128)S(1)} fusion(f32[8,8,135,128]{3,1,2,0:T(8,128)} %gather_fusion), kind=kLoop, calls=%fused_computation.2.clone.1 | loop fusion | flops 917504 | bytes 4718592 | tf_op jit(solution)/shard_map/while/body/eval_jaxpr/vmap()/add | solution.py:31
  72.3 6.1 %gather_fusion = f32[8,8,135,128]{3,1,2,0:T(8,128)} fusion(f32[8,8,192,128]{3,1,0,2:T(8,128)} %pad.13.clone.2, s32[8]{0:T(128)S(1)} %or_bitcast_fusion.4), kind=kCustom, calls=%fused_computation.clone.1 | custom fusion | bytes 8847488 | tf_op jit(solution)/shard_map/while/body/eval_jaxpr/vmap()/gather | solution.py:28
  78.3 13.6 %slice_add_fusion.9 = f32[8,1,128,128]{3,1,2,0:T(1,128)S(1)} fusion(f32[8,8,135,128]{3,1,2,0:T(8,128)} %gather_fusion), kind=kLoop, calls=%fused_computation.2.clone.1 | loop fusion | flops 917504 | bytes 4718592 | tf_op jit(solution)/shard_map/while/body/eval_jaxpr/vmap()/add | solution.py:31
  99.1 6.1 %gather_fusion = f32[8,8,135,128]{3,1,2,0:T(8,128)} fusion(f32[8,8,192,128]{3,1,0,2:T(8,128)} %pad.13.clone.2, s32[8]{0:T(128)S(1)} %or_bitcast_fusion.4), kind=kCustom, calls=%fused_computation.clone.1 | custom fusion | bytes 8847488 | tf_op jit(solution)/shard_map/while/body/eval_jaxpr/vmap()/gather | solution.py:28
  105.2 13.6 %slice_add_fusion.9 = f32[8,1,128,128]{3,1,2,0:T(1,128)S(1)} fusion(f32[8,8,135,128]{3,1,2,0:T(8,128)} %gather_fusion), kind=kLoop, calls=%fused_computation.2.clone.1 | loop fusion | flops 917504 | bytes 4718592 | tf_op jit(solution)/shard_map/while/body/eval_jaxpr/vmap()/add | solution.py:31
  126.0 6.1 %gather_fusion = f32[8,8,135,128]{3,1,2,0:T(8,128)} fusion(f32[8,8,192,128]{3,1,0,2:T(8,128)} %pad.13.clone.2, s32[8]{0:T(128)S(1)} %or_bitcast_fusion.4), kind=kCustom, calls=%fused_computation.clone.1 | custom fusion | bytes 8847488 | tf_op jit(solution)/shard_map/while/body/eval_jaxpr/vmap()/gather | solution.py:28
  132.1 13.6 %slice_add_fusion.9 = f32[8,1,128,128]{3,1,2,0:T(1,128)S(1)} fusion(f32[8,8,135,128]{3,1,2,0:T(8,128)} %gather_fusion), kind=kLoop, calls=%fused_computation.2.clone.1 | loop fusion | flops 917504 | bytes 4718592 | tf_op jit(solution)/shard_map/while/body/eval_jaxpr/vmap()/add | solution.py:31
  152.9 6.1 %gather_fusion = f32[8,8,135,128]{3,1,2,0:T(8,128)} fusion(f32[8,8,192,128]{3,1,0,2:T(8,128)} %pad.13.clone.2, s32[8]{0:T(128)S(1)} %or_bitcast_fusion.4), kind=kCustom, calls=%fused_computation.clone.1 | custom fusion | bytes 8847488 | tf_op jit(solution)/shard_map/while/body/eval_jaxpr/vmap()/gather | solution.py:28
  159.0 13.6 %slice_add_fusion.9 = f32[8,1,128,128]{3,1,2,0:T(1,128)S(1)} fusion(f32[8,8,135,128]{3,1,2,0:T(8,128)} %gather_fusion), kind=kLoop, calls=%fused_computation.2.clone.1 | loop fusion | flops 917504 | bytes 4718592 | tf_op jit(solution)/shard_map/while/body/eval_jaxpr/vmap()/add | solution.py:31
  179.8 6.1 %gather_fusion = f32[8,8,135,128]{3,1,2,0:T(8,128)} fusion(f32[8,8,192,128]{3,1,0,2:T(8,128)} %pad.13.clone.2, s32[8]{0:T(128)S(1)} %or_bitcast_fusion.4), kind=kCustom, calls=%fused_computation.clone.1 | custom fusion | bytes 8847488 | tf_op jit(solution)/shard_map/while/body/eval_jaxpr/vmap()/gather | solution.py:28
  185.9 13.6 %slice_add_fusion.9 = f32[8,1,128,128]{3,1,2,0:T(1,128)S(1)} fusion(f32[8,8,135,128]{3,1,2,0:T(8,128)} %gather_fusion), kind=kLoop, calls=%fused_computation.2.clone.1 | loop fusion | flops 917504 | bytes 4718592 | tf_op jit(solution)/shard_map/while/body/eval_jaxpr/vmap()/add | solution.py:31
  206.7 6.1 %gather_fusion = f32[8,8,135,128]{3,1,2,0:T(8,128)} fusion(f32[8,8,192,128]{3,1,0,2:T(8,128)} %pad.13.clone.2, s32[8]{0:T(128)S(1)} %or_bitcast_fusion.4), kind=kCustom, calls=%fused_computation.clone.1 | custom fusion | bytes 8847488 | tf_op jit(solution)/shard_map/while/body/eval_jaxpr/vmap()/gather | solution.py:28
  212.8 13.6 %slice_add_fusion.9 = f32[8,1,128,128]{3,1,2,0:T(1,128)S(1)} fusion(f32[8,8,135,128]{3,1,2,0:T(8,128)} %gather_fusion), kind=kLoop, calls=%fused_computation.2.clone.1 | loop fusion | flops 917504 | bytes 4718592 | tf_op jit(solution)/shard_map/while/body/eval_jaxpr/vmap()/add | solution.py:31
  230.4 48.6 %collective-permute-done = f32[64,64,128]{2,1,0:T(8,128)S(1)} collective-permute-done((f32[64,64,128]{2,1,0:T(8,128)S(1)}, f32[64,64,128]{2,1,0:T(8,128)S(1)}, u32[]{:S(2)}, u32[]{:S(2)}) %collective-permute-start) | collective-permute-done | bytes 2097184 | tf_op jit(solution)/shard_map/ppermute | solution.py:10
  282.4 37.3 %reduce-scatter.2.cloned.1.call-done = f32[8,64,128]{2,1,0:T(8,128)} async-done(((f32[64,64,128]{2,1,0:T(8,128)}), f32[8,64,128]{2,1,0:T(8,128)}) %reduce-scatter.2.cloned.1.call-update) | async-done | bytes 262160 | tf_op jit(solution)/shard_map/reduce_scatter | solution.py:40
  330.3 39.0 %psum.7 = f32[]{:T(128)} all-reduce(f32[]{:T(128)} %get-tuple-element.237), channel_id=1, replica_groups=mesh['gx'=8,'gy'=2,'gz'=2] {'gx','gy','gz'}, use_global_device_ids=true, to_apply=%region_6.7 | all-reduce | flops 1 | bytes 8 | tf_op jit(solution)/shard_map/psum | solution.py:68
  370.0 10.4 %all-gather.3.cloned.1.call-done = f32[64,64,128]{2,1,0:T(8,128)} async-done(((f32[8,64,128]{2,1,0:T(8,128)}), f32[64,64,128]{2,1,0:T(8,128)}) %all-gather.3.cloned.1.call-update) | async-done | bytes 2097168 | tf_op jit(solution)/shard_map/all_gather | solution.py:45
  385.1 91.6 %while.28 = (s32[]{:T(128)}, f32[16,64,128]{2,0,1:T(8,128)}, f32[8,8,8,16]{3,2,1,0:T(8,128)}, f32[8,8,128,128]{3,2,1,0:T(8,128)}, s32[8,8]{1,0:T(8,128)S(1)}, /*index=5*/s32[]{:T(128)}, s32[]{:T(128)}) while((s32[]{:T(128)}, f32[16,64,128]{2,0,1:T(8,128)}, f32[8,8,8,16]{3,2,1,0:T(8,128)}, f32[8,8,128,128]{3,2,1,0:T(8,128)}, ...), condition=%wide.region_4.5_spmd.clone, body=%wide.region_3.4_spmd.clone.sunk | while | flops 100925512 | bytes 14246655 | solution.py:64
  388.4 5.1 %stack.91 = f32[8,8,64,128]{3,0,1,2:T(8,128)S(1)} concatenate(f32[1,8,64,128]{3,0,1,2:T(1,128)} %bitcast.108, f32[1,8,64,128]{3,0,1,2:T(1,128)} %bitcast.107, f32[1,8,64,128]{3,0,1,2:T(1,128)} %bitcast.106, f32[1,8,64,128]{3,0,1,2:T(1,128)S(1)} %bitcast.105, f32[1,8,64,128]{3,0,1,2:T(1,128)S(1)} %bitcast.104, f32[1,8,64,128]{3,0,1,2:T(1,128)S(1)} %bitcast.103, ...), dimensions={0} | concatenate | bytes 4194304 | tf_op jit(solution)/shard_map/while/body/eval_jaxpr/vmap()/stack | solution.py:56
  399.6 5.1 %stack.91 = f32[8,8,64,128]{3,0,1,2:T(8,128)S(1)} concatenate(f32[1,8,64,128]{3,0,1,2:T(1,128)} %bitcast.108, f32[1,8,64,128]{3,0,1,2:T(1,128)} %bitcast.107, f32[1,8,64,128]{3,0,1,2:T(1,128)} %bitcast.106, f32[1,8,64,128]{3,0,1,2:T(1,128)S(1)} %bitcast.105, f32[1,8,64,128]{3,0,1,2:T(1,128)S(1)} %bitcast.104, f32[1,8,64,128]{3,0,1,2:T(1,128)S(1)} %bitcast.103, ...), dimensions={0} | concatenate | bytes 4194304 | tf_op jit(solution)/shard_map/while/body/eval_jaxpr/vmap()/stack | solution.py:56
  (120 shorter events, 167.6 us)
Async XLA Ops:
  7.2 312.5 %reduce-scatter.2.cloned.1.call-start = ((), (), s32[]{:S(2)}) async-start(), calls=%async_computation.1 | async-start | bytes 2359296 | tf_op jit(solution)/shard_map/reduce_scatter | solution.py:40
  228.9 90.7 %copy-start.1 = (f32[8,64,128]{2,1,0:T(8,128)S(1)}, f32[8,64,128]{2,1,0:T(8,128)}, u32[]{:S(2)}) copy-start(f32[8,64,128]{2,1,0:T(8,128)} %param.11) | copy-start | bytes 786436
  228.9 50.1 %collective-permute-start = (f32[64,64,128]{2,1,0:T(8,128)S(1)}, f32[64,64,128]{2,1,0:T(8,128)S(1)}, u32[]{:S(2)}, u32[]{:S(2)}) collective-permute-start(f32[64,64,128]{2,1,0:T(8,128)S(1)} %slice.162), channel_id=1, source_target_pairs={{2,0},{3,1},{6,4},{7,5},{10,8},{11,9},{14,12},{15,13},{18,16},{19,... | collective-permute-start | bytes 6291464 | tf_op jit(solution)/shard_map/ppermute | solution.py:10
  282.4 87.6 %all-gather.5.cloned.1.call-start = ((), (), s32[]{:S(2)}) async-start(), calls=%async_computation.3 | async-start | bytes 2359296 | tf_op jit(solution)/shard_map/all_gather | solution.py:44
  322.0 58.4 %all-gather.3.cloned.1.call-start = ((), (), s32[]{:S(2)}) async-start(), calls=%async_computation.2 | async-start | bytes 2359296 | tf_op jit(solution)/shard_map/all_gather | solution.py:45
  322.0 7.6 %collective-permute-start.1 = (f32[8,64,128]{2,1,0:T(8,128)}, f32[8,64,128]{2,1,0:T(8,128)S(1)}, u32[]{:S(2)}, u32[]{:S(2)}) collective-permute-start(f32[8,64,128]{2,1,0:T(8,128)} %get-tuple-element.238), channel_id=1, source_target_pairs={{0,2},{1,3},{4,6},{5,7},{8,10},{9,11},{12,14},{13,15},{16,18},{17,... | collective-permute-start | bytes 786440 | tf_op jit(solution)/shard_map/ppermute | solution.py:10
  329.6 0.7 copy-start
Sparse Core Ops, SparseCore 0:
  282.5 37.1 reduce-scatter.1
  322.1 27.9 all-gather.4
  351.7 28.7 all-gather.2
where the time goes:
time: 491 us; the launch traced here: 486 us
  local copies, waits for them, and re-layouts  161 us (33%)
  other arithmetic  120 us (24%)
  waiting for transfers between devices  101 us (21%)
  matrix products  44 us (9%)
  blocking collectives  39 us (8%)
  between operations  15.6 us (3%)
  starting transfers between devices  4.94 us (1%)
    add x8, other arithmetic, project_per_angle(): total = total + window[tap, tap:tap + 2 * rows]  109 us
    ppermute x2, waiting for transfers between devices, passed_along(): return lax.ppermute(x, axis, pairs)  52.8 us
    gather x8, local copies, waits for them, and re-layouts, project_per_angle(): window = lax.dynamic_slice_in_dim(plane, shift, 2 * rows + taps - 1, 1)  48.6 us
    another operation x8, local copies, waits for them, and re-layouts, backward_per_angle(): jnp.stack([window[taps - 1 - tap:taps - 1 - tap + rows] for tap in range(...  40.8 us
    psum x1, blocking collectives, body(): lax.psum(jnp.sum(resid_share * resid_share), ('gx', 'gy', 'gz')) / entries  39 us
    reduce_scatter x1, waiting for transfers between devices, body(): lax.psum_scatter(partial_value, 'gx', scatter_dimension=0, tiled=True)  37.3 us
    pad x8, local copies, waits for them, and re-layouts, project(): padded = jnp.pad(spread, ((0, 0), (0, 0), (rows, rows), (0, 0)))  28.4 us
    dot_general x8, matrix products, backward(): jnp.einsum('adc,adyz->cyz', wb, sheared, precision=lax.Precision.HIGHEST)  23.8 us
  transfers between devices with their start and end apart: 5, of which 4 were waited for; matrix products, arithmetic and copies ran while one was open for 0% of the time, Pallas kernels for 0%

commit v1 on v0

v1 whole, which is shorter than its diff:
```python
import functools

import jax
import jax.numpy as jnp
from jax import lax
from jax.experimental import pallas as pl
from jax.experimental.pallas import tpu as pltpu
from jax.sharding import PartitionSpec as P

SUB = 8
WIN = 16


def passed_along(x, axis, by):
    count = lax.axis_size(axis)
    pairs = [(i, i + by) for i in range(count) if 0 <= i + by < count]
    return lax.ppermute(x, axis, pairs)


def split(x):
    hi = x.astype(jnp.bfloat16)
    lo = (x - hi.astype(jnp.float32)).astype(jnp.bfloat16)
    return hi, lo


def toeplitz(flat):
    lead, lanes = flat.shape
    wide = jnp.broadcast_to(flat[:, None, :], (lead, SUB, lanes))
    rolled = pltpu.roll(wide, 0, 2, stride=1, stride_axis=1)
    return rolled.reshape(lead * SUB, lanes)


def dot(x, y):
    return jnp.dot(x, y, preferred_element_type=jnp.float32)


def forward_kernel(off_ref, w_ref, vol_ref, halo_ref, part_ref, ext, q, thi, tlo):
    cols, rows, depth = vol_ref.shape
    angles = w_ref.shape[0]
    ext[:, :rows] = vol_ref[...]
    ext[:, rows : 2 * rows] = halo_ref[...]
    ext[:, 2 * rows :] = jnp.zeros((cols, SUB, depth), jnp.float32)
    thi[...], tlo[...] = split(toeplitz(w_ref[...]))

    def block(j, carry):
        at = pl.multiple_of(j * SUB, SUB)
        hi, lo = split(ext[:, pl.ds(at, WIN), :].reshape(cols * WIN, depth))
        both = dot(thi[...], jnp.concatenate([hi, lo], axis=1))
        res = both[:, :depth] + both[:, depth:] + dot(tlo[...], hi)
        q[:, pl.ds(at, SUB), :] = res.reshape(angles, SUB, depth)
        return carry

    lax.fori_loop(0, 2 * rows // SUB, block, 0)

    def shift(a, carry):
        part_ref[a] = q[a, pl.ds(off_ref[a], rows), :]
        return carry

    lax.fori_loop(0, angles, shift, 0, unroll=4)


def backward_kernel(off_ref, w_ref, res_ref, up_ref, own_ref, ext, thi, tlo, rhs):
    angles, rows, depth = res_ref.shape
    cols = w_ref.shape[0]
    taps = WIN - SUB
    ext[:, :rows] = jnp.zeros((angles, rows, depth), jnp.float32)
    ext[:, rows : 2 * rows] = res_ref[...]
    ext[:, 2 * rows :] = jnp.zeros((angles, rows + SUB, depth), jnp.float32)
    thi[...], tlo[...] = split(toeplitz(w_ref[...]))

    def block(j, out_ref, base):
        at = pl.multiple_of(j * SUB, SUB)

        def gather(a, carry):
            start = rows + base + j * SUB - (taps - 1) - off_ref[a]
            hi, lo = split(ext[a, pl.ds(start, WIN), :])
            to = pl.multiple_of(a * WIN, WIN)
            rhs[pl.ds(to, WIN), :depth] = hi
            rhs[pl.ds(to, WIN), depth:] = lo
            return carry

        lax.fori_loop(0, angles, gather, 0, unroll=8)
        both = dot(thi[...], rhs[...])
        res = both[:, :depth] + both[:, depth:] + dot(tlo[...], rhs[:, :depth])
        out_ref[:, pl.ds(at, SUB), :] = res.reshape(cols, SUB, depth)

    @pl.loop(0, rows // SUB)
    def _(j):
        block(j, up_ref, rows)

    @pl.loop(0, rows // SUB)
    def _(j):
        block(j, own_ref, 0)


VMEM = pl.BlockSpec(memory_space=pltpu.VMEM)
SMEM = pl.BlockSpec(memory_space=pltpu.SMEM)


def body(volume, weights, offsets, measured):
    cols, rows, depth = volume.shape
    angles, taps, _ = weights.shape
    shifts = offsets[:, 0]
    halo = passed_along(volume, "gy", -1)
    pad = ((0, 0), (0, 0), (0, WIN - taps))
    w_fwd = jnp.pad(weights.transpose(0, 2, 1), pad).reshape(angles, cols * WIN)
    w_bwd = jnp.pad(weights[:, ::-1].transpose(2, 0, 1), pad).reshape(cols, angles * WIN)
    f32, bf16 = jnp.float32, jnp.bfloat16
    partial_value = pl.pallas_call(
        forward_kernel,
        out_shape=jax.ShapeDtypeStruct((angles, rows, depth), f32),
        in_specs=[SMEM, VMEM, VMEM, VMEM],
        out_specs=VMEM,
        scratch_shapes=[
            pltpu.VMEM((cols, 2 * rows + SUB, depth), f32),
            pltpu.VMEM((angles, 2 * rows, depth), f32),
            pltpu.VMEM((angles * SUB, cols * WIN), bf16),
            pltpu.VMEM((angles * SUB, cols * WIN), bf16),
        ],
    )(shifts, w_fwd, volume, halo)
    summed = lax.psum_scatter(partial_value, "gx", scatter_dimension=0, tiled=True)
    resid_share = summed - measured
    resid_all = lax.all_gather(resid_share, "gx", axis=0, tiled=True)
    share = jax.ShapeDtypeStruct((cols, rows, depth), f32)
    upper, own = pl.pallas_call(
        backward_kernel,
        out_shape=[share, share],
        in_specs=[SMEM, VMEM, VMEM],
        out_specs=[VMEM, VMEM],
        scratch_shapes=[
            pltpu.VMEM((angles, 3 * rows + SUB, depth), f32),
            pltpu.VMEM((cols * SUB, angles * WIN), bf16),
            pltpu.VMEM((cols * SUB, angles * WIN), bf16),
            pltpu.VMEM((angles * WIN, 2 * depth), bf16),
        ],
    )(shifts, w_bwd, resid_all)
    gradient = own + passed_along(upper, "gy", 1)
    entries = angles * rows * depth * lax.axis_size("gy") * lax.axis_size("gz")
    misfit = lax.psum(jnp.sum(resid_share * resid_share), ("gx", "gy", "gz")) / entries
    return (gradient, resid_share, misfit)


def solution(mesh):
    in_specs = (P("gx", "gy", "gz"), P(None, None, "gx"), P(None, "gx"), P("gx", "gy", "gz"))
    out_specs = (P("gx", "gy", "gz"), P("gx", "gy", "gz"), P())
    return jax.shard_map(body, mesh=mesh, in_specs=in_specs, out_specs=out_specs, check_vma=False)
```

time: 491 us -> 170 us (0.35)
  local copies, waits for them, and re-layouts: 161 us -> 3.55 us
  other arithmetic: 120 us -> 4.17 us
  matrix products: 44 us -> 0 us
  waiting for transfers between devices: 101 us -> 77.6 us
  Pallas kernels: 0 us -> 18.8 us
  blocking collectives: 39 us -> 45.4 us
    add x9 -> x1, other arithmetic: 112 us -> 1.89 us  [body(): gradient = own + passed_along(upper, 'gy', 1)]
    gather x16 -> x0, local copies, waits for them, and re-layouts: 56.4 us -> none  [the longest x8 48.6 us: project_per_angle(): window = lax.dynamic_slice_in_dim(plane, shift, 2 * rows + taps - 1, 1)]
    dot_general x16 -> x0, matrix products: 44 us -> none  [the longest x8 23.8 us: backward(): jnp.einsum('adc,adyz->cyz', wb, sheared, precision=lax.Precision.HIGHEST)]
    another operation x9 -> x0, local copies, waits for them, and re-layouts: 40.8 us -> none  [the longest x8 40.8 us: backward_per_angle(): jnp.stack([window[taps - 1 - tap:taps - 1 - tap + rows] for tap in range(...]
    ppermute x2, waiting for transfers between devices: 52.8 us -> 13.5 us  [passed_along(): return lax.ppermute(x, axis, pairs)]
    pad x8 -> x2, local copies, waits for them, and re-layouts: 28.4 us -> 0.06 us  [the longest x1 0.05 us: body(): jnp.pad(weights[:, ::-1].transpose(2, 0, 1), pad)]
    pallas_call x0 -> x2, Pallas kernels: none -> 18.8 us  [the longest x1 10.9 us: body(): pl.pallas_call(backward_kernel, out_shape=[share, share], in_specs=[SMEM,...]
    all_gather x2 -> x1, waiting for transfers between devices: 10.4 us -> 26.8 us  [body(): resid_all = lax.all_gather(resid_share, 'gx', axis=0, tiled=True)]
  transfers between devices with their start and end apart: 5 -> 4, of which waited for: 4 -> 3; matrix products, arithmetic and copies ran while one was open for 0% -> 2% of each run, Pallas kernels for 0% -> 0%
where the time goes in v1:
time: 170 us
  waiting for transfers between devices  77.6 us (46%)
  blocking collectives  45.4 us (27%)
  Pallas kernels  18.8 us (11%)
  between operations  15.9 us (9%)
  starting transfers between devices  4.77 us (3%)
  other arithmetic  4.17 us (2%)
  local copies, waits for them, and re-layouts  3.55 us (2%)
    psum x1, blocking collectives, body(): lax.psum(jnp.sum(resid_share * resid_share), ('gx', 'gy', 'gz')) / entries  45.4 us
    reduce_scatter x1, waiting for transfers between devices, body(): lax.psum_scatter(partial_value, 'gx', scatter_dimension=0, tiled=True)  37.2 us
    all_gather x1, waiting for transfers between devices, body(): resid_all = lax.all_gather(resid_share, 'gx', axis=0, tiled=True)  26.8 us
    ppermute x2, waiting for transfers between devices, passed_along(): return lax.ppermute(x, axis, pairs)  13.5 us
    pallas_call x1, Pallas kernels, body(): pl.pallas_call(backward_kernel, out_shape=[share, share], in_specs=[SMEM,...  10.9 us
    pallas_call x1, Pallas kernels, body(): pl.pallas_call(forward_kernel, out_shape=jax.ShapeDtypeStruct((angles, ro...  7.92 us
    ppermute x2, starting transfers between devices, passed_along(): return lax.ppermute(x, axis, pairs)  4.69 us
  transfers between devices with their start and end apart: 4, of which 3 were waited for; matrix products, arithmetic and copies ran while one was open for 2% of the time, Pallas kernels for 0%

profile of v1, /device:TPU:0, one launch (start us, length us, event | category | flops | bytes accessed | tf_op | source)
XLA Modules:
  0.0 170.1 jit_solution(11079352258602817798)
XLA Ops:
  7.2 0.0 reduce-scatter.2.cloned.1.call-start
  7.2 1.3 collective-permute-start
  8.5 0.9 copy.16
  9.4 0.7 copy.14.w_ref
  10.1 13.5 %collective-permute-done.halo_ref = f32[16,64,128]{2,1,0:T(8,128)S(1)} collective-permute-done((f32[16,64,128]{2,1,0:T(8,128)}, f32[16,64,128]{2,1,0:T(8,128)S(1)}, u32[]{:S(2)}, u32[]{:S(2)}) %collective-permute-start) | collective-permute-done | bytes 524320 | tf_op jit(solution)/shard_map/ppermute | solution.py:17
  23.6 0.0 copy-start
  23.6 0.8 copy-done
  24.4 7.9 %shard_map.67 = f32[64,64,128]{2,1,0:T(8,128)} custom-call(s32[64]{0:T(128)} %bitcast.7, f32[64,256]{1,0:T(8,128)} %copy.14.w_ref, f32[16,64,128]{2,1,0:T(8,128)} %vol_ref.1, f32[16,64,128]{2,1,0:T(8,128)} %copy-done), custom_call_target="tpu_custom_call" | custom-call | tf_op jit(solution)/shard_map/pallas_call | solution.py:109
  32.4 0.0 reduce-scatter.2.cloned.1.call-update
  32.4 0.0 all-gather.2.cloned.1.call-start
  32.4 37.2 %reduce-scatter.2.cloned.1.call-done = f32[8,64,128]{2,1,0:T(8,128)} async-done(((f32[64,64,128]{2,1,0:T(8,128)}), f32[8,64,128]{2,1,0:T(8,128)}) %reduce-scatter.2.cloned.1.call-update) | async-done | bytes 262160 | tf_op jit(solution)/shard_map/reduce_scatter | solution.py:121
  69.7 0.0 copy-done.2
  69.7 2.3 %multiply_reduce_fusion = (f32[]{:T(128)}, f32[8,64,128]{2,1,0:T(8,128)}) fusion(f32[8,64,128]{2,1,0:T(8,128)} %reduce-scatter.2.cloned.1.call-done, f32[8,64,128]{2,1,0:T(8,128)S(1)} %copy-done.2), kind=kLoop, calls=%fused_computation | loop fusion | flops 196607 | bytes 786436 | tf_op jit(solution)/shard_map/reduce_sum | solution.py:139
  71.9 0.0 all-gather.2.cloned.1.call-update
  72.0 0.0 copy-done.1
  72.0 0.2 copy.15
  72.2 0.1 pad.8.clone
  72.3 0.9 reshape.12.w_ref
  73.2 26.8 %all-gather.2.cloned.1.call-done.res_ref = f32[64,64,128]{2,1,0:T(8,128)} async-done(((f32[8,64,128]{2,1,0:T(8,128)}), f32[64,64,128]{2,1,0:T(8,128)}) %all-gather.2.cloned.1.call-update) | async-done | bytes 2097168 | tf_op jit(solution)/shard_map/all_gather | solution.py:123
  99.9 10.9 %shard_map.68 = (f32[16,64,128]{2,1,0:T(8,128)}, f32[16,64,128]{2,1,0:T(8,128)}) custom-call(s32[64]{0:T(128)} %bitcast.8, f32[16,1024]{1,0:T(8,128)} %reshape.12.w_ref, f32[64,64,128]{2,1,0:T(8,128)} %all-gather.2.cloned.1.call-done.res_ref), custom_call_target="tpu_custom_call" | custom-call | tf_op jit(solution)/shard_map/pallas_call | solution.py:125
  110.8 3.4 %collective-permute-start.1 = (f32[16,64,128]{2,1,0:T(8,128)}, f32[16,64,128]{2,1,0:T(8,128)S(1)}, u32[]{:S(2)}, u32[]{:S(2)}) collective-permute-start(f32[16,64,128]{2,1,0:T(8,128)} %get-tuple-element.6), channel_id=1, source_target_pairs={{0,2},{1,3},{4,6},{5,7},{8,10},{9,11},{12,14},{13,15},{16,18},{17,... | collective-permute-start | bytes 1572872 | tf_op jit(solution)/shard_map/ppermute | solution.py:17
  114.2 45.4 %psum.7 = f32[]{:T(128)} all-reduce(f32[]{:T(128)} %get-tuple-element.7), channel_id=1, replica_groups=mesh['gx'=8,'gy'=2,'gz'=2] {'gx','gy','gz'}, use_global_device_ids=true, to_apply=%region_2.3 | all-reduce | flops 1 | bytes 8 | tf_op jit(solution)/shard_map/psum | solution.py:139
  160.2 0.0 collective-permute-done.1
  160.2 1.9 %add.11 = f32[16,64,128]{2,1,0:T(8,128)} add(f32[16,64,128]{2,1,0:T(8,128)} %get-tuple-element.5, f32[16,64,128]{2,1,0:T(8,128)S(1)} %collective-permute-done.1) | non-fusion elementwise | flops 131072 | bytes 1572864 | tf_op jit(solution)/shard_map/add | solution.py:137
  (4 shorter events, 0.0 us)
Async XLA Ops:
  7.2 62.5 %reduce-scatter.2.cloned.1.call-start = ((), (), s32[]{:S(2)}) async-start(), calls=%async_computation.1 | async-start | bytes 2359296 | tf_op jit(solution)/shard_map/reduce_scatter | solution.py:121
  7.2 16.4 %collective-permute-start = (f32[16,64,128]{2,1,0:T(8,128)}, f32[16,64,128]{2,1,0:T(8,128)S(1)}, u32[]{:S(2)}, u32[]{:S(2)}) collective-permute-start(f32[16,64,128]{2,1,0:T(8,128)} %vol_ref.1), channel_id=1, source_target_pairs={{2,0},{3,1},{6,4},{7,5},{10,8},{11,9},{14,12},{15,13},{18,16},{19,... | collective-permute-start | bytes 1572872 | tf_op jit(solution)/shard_map/ppermute | solution.py:17
  23.6 0.8 copy-start
  24.4 45.2 %copy-start.2 = (f32[8,64,128]{2,1,0:T(8,128)S(1)}, f32[8,64,128]{2,1,0:T(8,128)}, u32[]{:S(2)}) copy-start(f32[8,64,128]{2,1,0:T(8,128)} %param.7) | copy-start | bytes 786436
  32.4 39.6 %copy-start.1 = (f32[64,8,16]{0,2,1:T(8,128)S(1)}, f32[64,8,16]{0,2,1:T(8,128)}, u32[]{:S(2)}) copy-start(f32[64,8,16]{0,2,1:T(8,128)} %param.5) | copy-start | bytes 98308
  32.4 67.5 %all-gather.2.cloned.1.call-start = ((), (), s32[]{:S(2)}) async-start(), calls=%async_computation.2 | async-start | bytes 2359296 | tf_op jit(solution)/shard_map/all_gather | solution.py:123
  110.8 49.4 %collective-permute-start.1 = (f32[16,64,128]{2,1,0:T(8,128)}, f32[16,64,128]{2,1,0:T(8,128)S(1)}, u32[]{:S(2)}, u32[]{:S(2)}) collective-permute-start(f32[16,64,128]{2,1,0:T(8,128)} %get-tuple-element.6), channel_id=1, source_target_pairs={{0,2},{1,3},{4,6},{5,7},{8,10},{9,11},{12,14},{13,15},{16,18},{17,... | collective-permute-start | bytes 1572872 | tf_op jit(solution)/shard_map/ppermute | solution.py:17
Sparse Core Ops, SparseCore 0:
  32.5 37.1 reduce-scatter.1
  72.1 27.7 all-gather.1

commit v2 on v1

v2 whole, which is shorter than its diff:
```python
import functools

import jax
import jax.numpy as jnp
from jax import lax
from jax.experimental import pallas as pl
from jax.experimental.pallas import tpu as pltpu
from jax.sharding import PartitionSpec as P

SUB = 8
WIN = 16
CHUNK = 2
SKEW = 2
PIECE = 2
MESH = pl.DeviceIdType.MESH


def split(x):
    hi = x.astype(jnp.bfloat16)
    lo = (x - hi.astype(jnp.float32)).astype(jnp.bfloat16)
    return hi, lo


def toeplitz(flat):
    lead, lanes = flat.shape
    wide = jnp.broadcast_to(flat[:, None, :], (lead, SUB, lanes))
    rolled = pltpu.roll(wide, 0, 2, stride=1, stride_axis=1)
    return rolled.reshape(lead * SUB, lanes)


def dot(x, y):
    return jnp.dot(x, y, preferred_element_type=jnp.float32)


def kernel(
    off_ref, wf_ref, wb_ref, vol_ref, meas_ref, grad_ref, resid_ref, mis_ref,
    ext, q, part, fhi, flo, bhi, blo, rbuf, lin, rin, sr, sl, rext, rhs, up, gbuf, mx, my, mz,
    halo_sem, swap_s, swap_r, right_s, right_r, left_s, left_r, tot_s, tot_r, grad_s, grad_r,
    mx_s, mx_r, my_s, my_r, mz_s, mz_r,
):
    cols, rows, depth = vol_ref.shape
    angles = wf_ref.shape[0]
    share = meas_ref.shape[0]
    taps = WIN - SUB
    sizes = {axis: lax.axis_size(axis) for axis in ("gx", "gy", "gz")}
    at_axis = {axis: lax.axis_index(axis) for axis in ("gx", "gy", "gz")}
    gx, gy = at_axis["gx"], at_axis["gy"]
    chips = sizes["gx"] // 2
    z, core = gx // 2, gx % 2
    partner = gx + 1 - 2 * core
    last_y = sizes["gy"] - 1
    chunks = angles // (2 * CHUNK)

    def remote(src, dst, send, recv, axis, to):
        return pltpu.make_async_remote_copy(
            src_ref=src, dst_ref=dst, send_sem=send, recv_sem=recv,
            device_id={axis: to}, device_id_type=MESH,
        )

    barrier = pltpu.get_barrier_semaphore()
    total_peers = 0
    for axis, size in sizes.items():
        for step in range(1, size):
            to = lax.rem(at_axis[axis] + step, size)
            pl.semaphore_signal(barrier, inc=1, device_id={axis: to}, device_id_type=MESH)
        total_peers += size - 1
    pl.semaphore_wait(barrier, total_peers)

    halo = remote(
        vol_ref, ext.at[:, pl.ds(rows, rows), :], halo_sem.at[0], halo_sem.at[1], "gy",
        lax.rem(gy + last_y, last_y + 1),
    )

    @pl.when(gy > 0)
    def _():
        halo.start()

    @pl.when(gy == last_y)
    def _():
        ext[:, rows : 2 * rows] = jnp.zeros((cols, rows, depth), jnp.float32)

    ext[:, :rows] = vol_ref[...]
    ext[:, 2 * rows :] = jnp.zeros((cols, SUB, depth), jnp.float32)
    fhi[...], flo[...] = split(toeplitz(wf_ref[...]))
    bhi[...], blo[...] = split(toeplitz(wb_ref[...]))
    rext[:, :rows] = jnp.zeros((angles, rows, depth), jnp.float32)
    rext[:, 2 * rows :] = jnp.zeros((angles, rows + SUB, depth), jnp.float32)

    @pl.when(z == 0)
    def _():
        lin[...] = jnp.zeros_like(lin)

    @pl.when(z == chips - 1)
    def _():
        rin[...] = jnp.zeros_like(rin)

    def forward(j):
        at = pl.multiple_of(j * SUB, SUB)
        hi, lo = split(ext[:, pl.ds(at, WIN), :].reshape(cols * WIN, depth))
        both = dot(fhi[...], jnp.concatenate([hi, lo], axis=1))
        res = both[:, :depth] + both[:, depth:] + dot(flo[...], hi)
        q[:, pl.ds(at, SUB), :] = res.reshape(angles, SUB, depth)

    @pl.loop(0, rows // SUB - 1)
    def _(j):
        forward(j)

    @pl.when(gy < last_y)
    def _():
        halo.wait_recv()

    @pl.loop(rows // SUB - 1, 2 * rows // SUB)
    def _(j):
        forward(j)

    def first_angle(k, side):
        m = k * CHUNK
        return (2 * (m // share) + side) * share + m % share

    def span(k, side):
        return pl.ds(first_angle(k, side), CHUNK)

    def shift(k, side):
        for step in range(CHUNK):
            a = first_angle(k, side) + step
            part[a] = q[a, pl.ds(off_ref[a], rows), :]

    def swap(k):
        return remote(
            part.at[span(k, 1 - core)], rbuf.at[pl.ds(k * CHUNK, CHUNK)],
            swap_s.at[k], swap_r.at[k], "gx", partner,
        )

    @pl.loop(0, chunks)
    def _(k):
        shift(k, 1 - core)
        swap(k).start()

    @pl.loop(0, chunks)
    def _(k):
        shift(k, core)

    mine = pl.ds(gx * share, share)
    part[mine] = part[mine] - meas_ref[...]

    def chunk(k):
        return pl.ds(k * CHUNK, CHUNK)

    def go_right(k):
        return remote(
            sr.at[chunk(k)], lin.at[chunk(k)], right_s.at[k], right_r.at[k], "gx",
            lax.rem(gx + 2, sizes["gx"]),
        )

    def go_left(k):
        return remote(
            sl.at[chunk(k)], rin.at[chunk(k)], left_s.at[k], left_r.at[k], "gx",
            lax.rem(gx + sizes["gx"] - 2, sizes["gx"]),
        )

    def totals(k, side):
        where = rext.at[span(k, side), pl.ds(rows, rows), :]
        return remote(where, where, tot_s.at[k], tot_r.at[k], "gx", partner)

    from_right = chips - 1 - z

    def inside(k):
        return (k >= 0) & (k < chunks)

    @pl.loop(0, chunks + SKEW * (chips - 1))
    def _(t):
        k_add = t - SKEW * jnp.minimum(z, from_right)
        k_right = t - SKEW * z
        k_left = t - SKEW * from_right
        k_total = t - SKEW * jnp.maximum(z, from_right)

        @pl.when(inside(k_add))
        def _():
            swap(k_add).wait_recv()
            part[span(k_add, core)] = part[span(k_add, core)] + rbuf[chunk(k_add)]

        @pl.when(inside(k_right))
        def _():
            @pl.when(z > 0)
            def _():
                go_right(k_right).wait_recv()

            @pl.when(z < chips - 1)
            def _():
                sr[chunk(k_right)] = lin[chunk(k_right)] + part[span(k_right, core)]
                go_right(k_right).start()

        @pl.when(inside(k_left))
        def _():
            @pl.when(z < chips - 1)
            def _():
                go_left(k_left).wait_recv()

            @pl.when(z > 0)
            def _():
                sl[chunk(k_left)] = rin[chunk(k_left)] + part[span(k_left, core)]
                go_left(k_left).start()

        @pl.when(inside(k_total))
        def _():
            k = k_total
            rext[span(k, core), rows : 2 * rows, :] = (
                lin[chunk(k)] + part[span(k, core)] + rin[chunk(k)]
            )
            totals(k, core).start()

    owned = rext[mine, rows : 2 * rows, :]
    resid_ref[...] = owned
    tile = jnp.sum((owned * owned).reshape(share * rows // SUB, SUB, depth), axis=0)

    def spread(buf, send, recv, axis):
        size, me = sizes[axis], at_axis[axis]
        out = []
        for step in range(1, size):
            to = lax.rem(me + step, size)
            out.append(remote(buf.at[me], buf.at[me], send.at[step - 1], recv.at[step - 1], axis, to))
        return out

    def begin(buf, value, copies):
        buf[copies[0]] = value
        for copy in copies[1]:
            copy.start()

    def finish(buf, copies):
        for copy in copies:
            copy.wait()
        return jnp.sum(buf[...], axis=0)

    over_x = spread(mx, mx_s, mx_r, "gx")
    over_y = spread(my, my_s, my_r, "gy")
    over_z = spread(mz, mz_s, mz_r, "gz")
    begin(mx, tile, (at_axis["gx"], over_x))

    @pl.loop(0, chunks)
    def _(k):
        totals(k, 1 - core).wait_recv()

    def backward(j, out_ref, base):
        at = pl.multiple_of(j * SUB, SUB)

        def gather(a, carry):
            start = rows + base + j * SUB - (taps - 1) - off_ref[a]
            hi, lo = split(rext[a, pl.ds(start, WIN), :])
            to = pl.multiple_of(a * WIN, WIN)
            rhs[pl.ds(to, WIN), :depth] = hi
            rhs[pl.ds(to, WIN), depth:] = lo
            return carry

        lax.fori_loop(0, angles, gather, 0, unroll=8)
        both = dot(bhi[...], rhs[...])
        res = both[:, :depth] + both[:, depth:] + dot(blo[...], rhs[:, :depth])
        out_ref[:, pl.ds(at, SUB), :] = res.reshape(cols, SUB, depth)

    tall = PIECE * SUB
    pieces = rows // tall

    def give(p):
        where = pl.ds(pl.multiple_of(p * tall, tall), tall)
        return remote(
            up.at[:, where, :], gbuf.at[:, where, :], grad_s.at[p], grad_r.at[p], "gy",
            lax.rem(gy + 1, last_y + 1),
        )

    @pl.when(gy < last_y)
    def _():
        @pl.loop(0, pieces)
        def _(p):
            @pl.loop(0, PIECE)
            def _(b):
                backward(p * PIECE + b, up, rows)

            give(p).start()

    begin(my, finish(mx, over_x), (at_axis["gy"], over_y))

    @pl.loop(0, rows // SUB // 2)
    def _(j):
        backward(j, grad_ref, 0)

    begin(mz, finish(my, over_y), (at_axis["gz"], over_z))

    @pl.loop(rows // SUB // 2, rows // SUB)
    def _(j):
        backward(j, grad_ref, 0)

    mis_ref[...] = finish(mz, over_z)

    @pl.when(gy > 0)
    def _():
        @pl.loop(0, pieces)
        def _(p):
            give(p).wait_recv()
            where = pl.ds(pl.multiple_of(p * tall, tall), tall)
            grad_ref[:, where, :] = grad_ref[:, where, :] + gbuf[:, where, :]

        halo.wait_send()

    @pl.when(gy < last_y)
    def _():
        @pl.loop(0, pieces)
        def _(p):
            give(p).wait_send()

    @pl.loop(0, chunks)
    def _(k):
        swap(k).wait_send()
        totals(k, core).wait_send()

        @pl.when(z < chips - 1)
        def _():
            go_right(k).wait_send()

        @pl.when(z > 0)
        def _():
            go_left(k).wait_send()


VMEM = pl.BlockSpec(memory_space=pltpu.VMEM)
SMEM = pl.BlockSpec(memory_space=pltpu.SMEM)


def body(volume, weights, offsets, measured):
    cols, rows, depth = volume.shape
    angles, taps, _ = weights.shape
    share = measured.shape[0]
    shifts = offsets[:, 0]
    pad = ((0, 0), (0, 0), (0, WIN - taps))
    w_fwd = jnp.pad(weights.transpose(0, 2, 1), pad).reshape(angles, cols * WIN)
    w_bwd = jnp.pad(weights[:, ::-1].transpose(2, 0, 1), pad).reshape(cols, angles * WIN)
    f32, bf16 = jnp.float32, jnp.bfloat16
    half = angles // 2
    chunks = half // CHUNK
    sizes = [lax.axis_size(axis) for axis in ("gx", "gy", "gz")]
    dma = pltpu.SemaphoreType.DMA
    scratch = [
        pltpu.VMEM((cols, 2 * rows + SUB, depth), f32),
        pltpu.VMEM((angles, 2 * rows, depth), f32),
        pltpu.VMEM((angles, rows, depth), f32),
        pltpu.VMEM((angles * SUB, cols * WIN), bf16),
        pltpu.VMEM((angles * SUB, cols * WIN), bf16),
        pltpu.VMEM((cols * SUB, angles * WIN), bf16),
        pltpu.VMEM((cols * SUB, angles * WIN), bf16),
    ]
    scratch += [pltpu.VMEM((half, rows, depth), f32)] * 5
    scratch += [
        pltpu.VMEM((angles, 3 * rows + SUB, depth), f32),
        pltpu.VMEM((angles * WIN, 2 * depth), bf16),
        pltpu.VMEM((cols, rows, depth), f32),
        pltpu.VMEM((cols, rows, depth), f32),
    ]
    scratch += [pltpu.VMEM((size, SUB, depth), f32) for size in sizes]
    scratch += [dma((2,))]
    scratch += [dma((chunks,))] * 8
    scratch += [dma((rows // (SUB * PIECE),))] * 2
    for size in sizes:
        scratch += [dma((size - 1,))] * 2
    gradient, resid_share, tile = pl.pallas_call(
        kernel,
        out_shape=[
            jax.ShapeDtypeStruct((cols, rows, depth), f32),
            jax.ShapeDtypeStruct((share, rows, depth), f32),
            jax.ShapeDtypeStruct((SUB, depth), f32),
        ],
        in_specs=[SMEM, VMEM, VMEM, VMEM, VMEM],
        out_specs=[VMEM, VMEM, VMEM],
        scratch_shapes=scratch,
        compiler_params=pltpu.CompilerParams(collective_id=0, has_side_effects=True),
    )(shifts, w_fwd, w_bwd, volume, measured)
    entries = angles * rows * depth * sizes[1] * sizes[2]
    misfit = jnp.sum(tile) / entries
    return (gradient, resid_share, misfit)


def solution(mesh):
    in_specs = (P("gx", "gy", "gz"), P(None, None, "gx"), P(None, "gx"), P("gx", "gy", "gz"))
    out_specs = (P("gx", "gy", "gz"), P("gx", "gy", "gz"), P())
    return jax.shard_map(body, mesh=mesh, in_specs=in_specs, out_specs=out_specs, check_vma=False)
```

time: 170 us -> 87.2 us (0.51)
  waiting for transfers between devices: 77.6 us -> 0 us
  Pallas kernels: 18.8 us -> 77.6 us
  blocking collectives: 45.4 us -> 0 us
  between operations: 15.9 us -> 2.46 us
  starting transfers between devices: 4.77 us -> 0 us
  other arithmetic: 4.17 us -> 1.28 us
  local copies, waits for them, and re-layouts: 3.55 us -> 5.51 us
    pallas_call x2 -> x1, Pallas kernels: 18.8 us -> 77.6 us  [body(): pl.pallas_call(kernel, out_shape=[jax.ShapeDtypeStruct((cols, rows, depth...]
    psum x1 -> x0, blocking collectives: 45.4 us -> none  [body(): lax.psum(jnp.sum(resid_share * resid_share), ('gx', 'gy', 'gz')) / entries]
    reduce_scatter x1 -> x0, waiting for transfers between devices: 37.2 us -> none  [body(): lax.psum_scatter(partial_value, 'gx', scatter_dimension=0, tiled=True)]
    all_gather x1 -> x0, waiting for transfers between devices: 26.8 us -> none  [body(): resid_all = lax.all_gather(resid_share, 'gx', axis=0, tiled=True)]
    ppermute x2 -> x0, waiting for transfers between devices: 13.5 us -> none  [passed_along(): return lax.ppermute(x, axis, pairs)]
    ppermute x2 -> x0, starting transfers between devices: 4.69 us -> none  [passed_along(): return lax.ppermute(x, axis, pairs)]
    unnamed x8, local copies, waits for them, and re-layouts: 1.87 us -> 3.83 us
    add x1 -> x0, other arithmetic: 1.89 us -> none  [body(): gradient = own + passed_along(upper, 'gy', 1)]
  transfers between devices with their start and end apart: 4 -> 0, of which waited for: 3 -> 0; matrix products, arithmetic and copies ran while one was open for 2% -> 0% of each run, Pallas kernels for 0% -> 0%
where the time goes in v2:
time: 87.2 us; the launch traced here: 86.9 us
  Pallas kernels  77.6 us (89%)
  local copies, waits for them, and re-layouts  5.51 us (6%)
  between operations  2.46 us (3%)
  other arithmetic  1.28 us (1%)
    pallas_call x1, Pallas kernels, body(): pl.pallas_call(kernel, out_shape=[jax.ShapeDtypeStruct((cols, rows, depth...  77.6 us
    unnamed x8, local copies, waits for them, and re-layouts  3.83 us

profile of v2, /device:TPU:0, one launch (start us, length us, event | category | flops | bytes accessed | tf_op | source)
XLA Modules:
  0.0 86.9 jit_solution(9321700234386185424)
XLA Ops:
  0.6 0.9 copy.12
  1.5 0.0 copy-start.1
  1.5 0.7 copy.11.wf_ref
  2.2 0.1 copy-done.1
  2.4 0.2 copy.13
  2.6 0.1 pad.9.clone
  2.6 0.9 %reshape.13.wb_ref = f32[16,1024]{1,0:T(8,128)} reshape(f32[16,64,16]{2,1,0:T(8,128)S(1)} %pad.9.clone) | data formatting | bytes 131072 | tf_op jit(solution)/shard_map/reshape | solution.py:334
  3.5 77.6 %shard_map.67 = (f32[16,64,128]{2,1,0:T(8,128)}, f32[8,64,128]{2,1,0:T(8,128)}, f32[8,128]{1,0:T(8,128)}) custom-call(s32[64]{0:T(128)} %bitcast.7, f32[64,256]{1,0:T(8,128)} %copy.11.wf_ref, f32[16,1024]{1,0:T(8,128)} %reshape.13.wb_ref, f32[16,64,128]{2,1,0:T(8,128)} %vol_ref.1, f32[8,64,128]{2,1,0:T(8,128)} %meas_ref.1), custom_call_target="tpu_custom_call" | custom-call | tf_op jit(solution)/shard_map/pallas_call | solution.py:362
  81.1 1.3 %reduce_sum.9 = f32[]{:T(128)} reduce(f32[8,128]{1,0:T(8,128)} %get-tuple-element.8, f32[]{:T(128)} %constant.2.clone.1), dimensions={0,1}, to_apply=%region_0.1 | reduce | flops 1023 | bytes 4104 | tf_op jit(solution)/shard_map/reduce_sum | solution.py:375
  83.1 0.0 copy-start
  83.1 1.9 %copy.16 = f32[16,64,128]{2,1,0:T(8,128)} copy(f32[16,64,128]{2,1,0:T(8,128)} %get-tuple-element.12) | data formatting | bytes 1048576
  85.0 0.0 copy-done
  85.0 0.7 copy.17
  (2 shorter events, 0.0 us)
Async XLA Ops:
  1.5 0.8 copy-start.1
  83.1 1.9 %copy-start = (f32[8,64,128]{2,1,0:T(8,128)S(1)}, f32[8,64,128]{2,1,0:T(8,128)}, u32[]{:S(2)}) copy-start(f32[8,64,128]{2,1,0:T(8,128)} %get-tuple-element.13) | copy-start | bytes 786436

commit v3 on v2

v3 whole, which is shorter than its diff:
```python
import functools

import jax
import jax.numpy as jnp
from jax import lax
from jax.experimental import pallas as pl
from jax.experimental.pallas import tpu as pltpu
from jax.sharding import PartitionSpec as P

SUB = 8
WIN = 16
CHUNK = 2
SKEW = 2
LAG = 2
PIECE = 2
GROUP = 16
MESH = pl.DeviceIdType.MESH


def split(x):
    hi = x.astype(jnp.bfloat16)
    lo = (x - hi.astype(jnp.float32)).astype(jnp.bfloat16)
    return hi, lo


def toeplitz(flat):
    lead, lanes = flat.shape
    wide = jnp.broadcast_to(flat[:, None, :], (lead, SUB, lanes))
    rolled = pltpu.roll(wide, 0, 2, stride=1, stride_axis=1)
    return rolled.reshape(lead * SUB, lanes)


def dot(x, y):
    return jnp.dot(x, y, preferred_element_type=jnp.float32)


def kernel(
    off_ref, wf_ref, wb_ref, vol_ref, meas_ref, grad_ref, resid_ref, mis_ref,
    ext, q, part, fhi, flo, bhi, blo, rbuf, lin, rin, sr, sl, rext, near, mx, myz,
    halo_s, halo_r, swap_s, swap_r, right_s, right_r, left_s, left_r, tot_s, tot_r,
    bef_s, bef_r, pass_s, pass_r, mx_s, mx_r, myz_s, myz_r,
):
    cols, rows, depth = vol_ref.shape
    angles = wf_ref.shape[0]
    share = meas_ref.shape[0]
    taps = WIN - SUB
    sizes = {axis: lax.axis_size(axis) for axis in ("gx", "gy", "gz")}
    at_axis = {axis: lax.axis_index(axis) for axis in ("gx", "gy", "gz")}
    gx, gy = at_axis["gx"], at_axis["gy"]
    chips = sizes["gx"] // 2
    z, core = gx // 2, gx % 2
    partner = gx + 1 - 2 * core
    last_y = sizes["gy"] - 1
    chunks = angles // (2 * CHUNK)

    def remote(src, dst, send, recv, to):
        return pltpu.make_async_remote_copy(
            src_ref=src, dst_ref=dst, send_sem=send, recv_sem=recv,
            device_id=to, device_id_type=MESH,
        )

    def ahead(axis, step):
        return lax.rem(at_axis[axis] + step, sizes[axis])

    over_gx = [{"gx": ahead("gx", step)} for step in range(1, sizes["gx"])]
    over_yz = [
        {"gy": ahead("gy", i), "gz": ahead("gz", j)}
        for i in range(sizes["gy"])
        for j in range(sizes["gz"])
        if i or j
    ]
    barrier = pltpu.get_barrier_semaphore()
    for to in over_gx + over_yz:
        pl.semaphore_signal(barrier, inc=1, device_id=to, device_id_type=MESH)
    pl.semaphore_wait(barrier, len(over_gx) + len(over_yz))

    tall = PIECE * SUB
    pieces = rows // tall
    below = {"gy": ahead("gy", last_y)}
    above = {"gy": ahead("gy", 1)}

    def halo(p):
        at = pl.multiple_of(p * tall, tall)
        return remote(
            vol_ref.at[:, pl.ds(at, tall), :], ext.at[:, pl.ds(rows + at, tall), :],
            halo_s.at[p], halo_r.at[p], below,
        )

    @pl.when(gy > 0)
    def _():
        @pl.loop(0, pieces)
        def _(p):
            halo(p).start()

    @pl.when(gy == last_y)
    def _():
        ext[:, rows : 2 * rows] = jnp.zeros((cols, rows, depth), jnp.float32)

    ext[:, :rows] = vol_ref[...]
    ext[:, 2 * rows :] = jnp.zeros((cols, SUB, depth), jnp.float32)
    fhi[...], flo[...] = split(toeplitz(wf_ref[...]))
    span_k = GROUP * WIN
    for g in range(angles // GROUP):
        wide = toeplitz(wb_ref[:, g * span_k : (g + 1) * span_k])
        bhi[g], blo[g] = split(wide)
    near[:, 2 * rows :] = jnp.zeros((GROUP, SUB, depth), jnp.float32)
    grad_ref[...] = jnp.zeros_like(grad_ref)

    @pl.when(gy == 0)
    def _():
        rext[:, :rows] = jnp.zeros((angles, rows, depth), jnp.float32)

    @pl.when(z == 0)
    def _():
        lin[...] = jnp.zeros_like(lin)

    @pl.when(z == chips - 1)
    def _():
        rin[...] = jnp.zeros_like(rin)

    def forward(j):
        at = pl.multiple_of(j * SUB, SUB)
        hi, lo = split(ext[:, pl.ds(at, WIN), :].reshape(cols * WIN, depth))
        both = dot(fhi[...], jnp.concatenate([hi, lo], axis=1))
        res = both[:, :depth] + both[:, depth:] + dot(flo[...], hi)
        q[:, pl.ds(at, SUB), :] = res.reshape(angles, SUB, depth)

    @pl.loop(0, rows // SUB - 1)
    def _(j):
        forward(j)

    @pl.loop(0, pieces)
    def _(p):
        @pl.when(gy < last_y)
        def _():
            halo(p).wait_recv()

        @pl.loop(0, PIECE)
        def _(b):
            forward(rows // SUB - 1 + p * PIECE + b)

    forward(2 * rows // SUB - 1)

    def first_angle(k, side):
        m = k * CHUNK
        return (2 * (m // share) + side) * share + m % share

    def span(k, side):
        return pl.ds(first_angle(k, side), CHUNK)

    def shift(k, side):
        for step in range(CHUNK):
            a = first_angle(k, side) + step
            part[a] = q[a, pl.ds(off_ref[a], rows), :]

    def swap(k):
        return remote(
            part.at[span(k, 1 - core)], rbuf.at[pl.ds(k * CHUNK, CHUNK)],
            swap_s.at[k], swap_r.at[k], {"gx": partner},
        )

    @pl.loop(0, chunks)
    def _(k):
        shift(k, 1 - core)
        swap(k).start()

    @pl.loop(0, chunks)
    def _(k):
        shift(k, core)

    mine = pl.ds(gx * share, share)
    part[mine] = part[mine] - meas_ref[...]

    def chunk(k):
        return pl.ds(k * CHUNK, CHUNK)

    def go_right(k):
        return remote(
            sr.at[chunk(k)], lin.at[chunk(k)], right_s.at[k], right_r.at[k],
            {"gx": ahead("gx", 2)},
        )

    def go_left(k):
        return remote(
            sl.at[chunk(k)], rin.at[chunk(k)], left_s.at[k], left_r.at[k],
            {"gx": ahead("gx", sizes["gx"] - 2)},
        )

    def totals(k, side):
        where = rext.at[span(k, side), pl.ds(rows, rows), :]
        return remote(where, where, tot_s.at[k], tot_r.at[k], {"gx": partner})

    def climb(k):
        return remote(
            rext.at[span(k, core), pl.ds(rows, rows), :], rext.at[span(k, core), pl.ds(0, rows), :],
            bef_s.at[k], bef_r.at[k], above,
        )

    def passed(k, side):
        where = rext.at[span(k, side), pl.ds(0, rows), :]
        return remote(where, where, pass_s.at[k], pass_r.at[k], {"gx": partner})

    def spread(buf, me, send, recv, peers):
        return [
            remote(buf.at[me], buf.at[me], send.at[i], recv.at[i], to)
            for i, to in enumerate(peers)
        ]

    me_yz = gy * sizes["gz"] + at_axis["gz"]
    tiles_x = spread(mx, gx, mx_s, mx_r, over_gx)
    tiles_yz = spread(myz, me_yz, myz_s, myz_r, over_yz)
    per_group = GROUP // (2 * CHUNK)
    per_step = rows // SUB // per_group

    def backward(g, j):
        at = pl.multiple_of(j * SUB, SUB)
        windows = []
        for i in range(GROUP):
            a = g * GROUP + i
            windows.append(near[i, pl.ds(rows + j * SUB - (taps - 1) - off_ref[a], WIN), :])
        hi, lo = split(jnp.concatenate(windows, axis=0))
        both = dot(bhi[g], jnp.concatenate([hi, lo], axis=1))
        res = both[:, :depth] + both[:, depth:] + dot(blo[g], hi)
        grad_ref[:, pl.ds(at, SUB), :] += res.reshape(cols, SUB, depth)

    from_right = chips - 1 - z

    def inside(k):
        return (k >= 0) & (k < chunks)

    far = jnp.maximum(z, from_right)

    @pl.loop(0, chunks + SKEW * (chips - 1) + LAG + 1 + per_group)
    def _(t):
        k_add = t - SKEW * jnp.minimum(z, from_right)
        k_right = t - SKEW * z
        k_left = t - SKEW * from_right
        k_total = t - SKEW * far
        k_before = k_total - LAG
        k_back = k_before - 1 - per_group

        @pl.when(inside(k_add))
        def _():
            swap(k_add).wait_recv()
            part[span(k_add, core)] = part[span(k_add, core)] + rbuf[chunk(k_add)]

        @pl.when(inside(k_right))
        def _():
            @pl.when(z > 0)
            def _():
                go_right(k_right).wait_recv()

            @pl.when(z < chips - 1)
            def _():
                sr[chunk(k_right)] = lin[chunk(k_right)] + part[span(k_right, core)]
                go_right(k_right).start()

        @pl.when(inside(k_left))
        def _():
            @pl.when(z < chips - 1)
            def _():
                go_left(k_left).wait_recv()

            @pl.when(z > 0)
            def _():
                sl[chunk(k_left)] = rin[chunk(k_left)] + part[span(k_left, core)]
                go_left(k_left).start()

        @pl.when(inside(k_total))
        def _():
            k = k_total
            rext[span(k, core), rows : 2 * rows, :] = (
                lin[chunk(k)] + part[span(k, core)] + rin[chunk(k)]
            )
            totals(k, core).start()

            @pl.when(gy < last_y)
            def _():
                climb(k).start()

        @pl.when(k_total == chunks)
        def _():
            owned = rext[mine, rows : 2 * rows, :]
            resid_ref[...] = owned
            mx[gx] = jnp.sum((owned * owned).reshape(share * rows // SUB, SUB, depth), axis=0)
            for copy in tiles_x:
                copy.start()

        @pl.when(inside(k_before) & (gy > 0))
        def _():
            climb(k_before).wait_recv()
            passed(k_before, core).start()

        @pl.when(k_total == chunks + LAG)
        def _():
            for copy in tiles_x:
                copy.wait()
            myz[me_yz] = jnp.sum(mx[...], axis=0)
            for copy in tiles_yz:
                copy.start()

        @pl.when(inside(k_back))
        def _():
            g = k_back // per_group
            step = k_back % per_group

            @pl.when(step == 0)
            def _():
                @pl.loop(0, per_group)
                def _(i):
                    totals(g * per_group + i, 1 - core).wait_recv()

                    @pl.when(gy > 0)
                    def _():
                        passed(g * per_group + i, 1 - core).wait_recv()

                near[:, : 2 * rows] = rext[pl.ds(g * GROUP, GROUP)]

            @pl.loop(0, per_step)
            def _(i):
                backward(g, step * per_step + i)

    for copy in tiles_yz:
        copy.wait()
    entries = angles * rows * depth * sizes["gy"] * sizes["gz"]
    mis_ref[0, 0] = jnp.sum(jnp.sum(myz[...], axis=0)) * (1.0 / entries)

    @pl.when(gy > 0)
    def _():
        @pl.loop(0, pieces)
        def _(p):
            halo(p).wait_send()

        @pl.loop(0, chunks)
        def _(k):
            passed(k, core).wait_send()

    @pl.loop(0, chunks)
    def _(k):
        swap(k).wait_send()
        totals(k, core).wait_send()

        @pl.when(gy < last_y)
        def _():
            climb(k).wait_send()

        @pl.when(z < chips - 1)
        def _():
            go_right(k).wait_send()

        @pl.when(z > 0)
        def _():
            go_left(k).wait_send()


VMEM = pl.BlockSpec(memory_space=pltpu.VMEM)
SMEM = pl.BlockSpec(memory_space=pltpu.SMEM)


def body(volume, weights, offsets, measured):
    cols, rows, depth = volume.shape
    angles, taps, _ = weights.shape
    share = measured.shape[0]
    shifts = offsets[:, 0]
    pad = ((0, 0), (0, 0), (0, WIN - taps))
    w_fwd = jnp.pad(weights.transpose(0, 2, 1), pad).reshape(angles, cols * WIN)
    w_bwd = jnp.pad(weights[:, ::-1].transpose(2, 0, 1), pad).reshape(cols, angles * WIN)
    f32, bf16 = jnp.float32, jnp.bfloat16
    half = angles // 2
    chunks = half // CHUNK
    sizes = [lax.axis_size(axis) for axis in ("gx", "gy", "gz")]
    dma = pltpu.SemaphoreType.DMA
    scratch = [
        pltpu.VMEM((cols, 2 * rows + SUB, depth), f32),
        pltpu.VMEM((angles, 2 * rows, depth), f32),
        pltpu.VMEM((angles, rows, depth), f32),
        pltpu.VMEM((angles * SUB, cols * WIN), bf16),
        pltpu.VMEM((angles * SUB, cols * WIN), bf16),
        pltpu.VMEM((angles // GROUP, cols * SUB, GROUP * WIN), bf16),
        pltpu.VMEM((angles // GROUP, cols * SUB, GROUP * WIN), bf16),
    ]
    scratch += [pltpu.VMEM((half, rows, depth), f32)] * 5
    scratch += [
        pltpu.VMEM((angles, 2 * rows, depth), f32),
        pltpu.VMEM((GROUP, 2 * rows + SUB, depth), f32),
        pltpu.VMEM((sizes[0], SUB, depth), f32),
        pltpu.VMEM((sizes[1] * sizes[2], SUB, depth), f32),
    ]
    scratch += [dma((rows // (SUB * PIECE),))] * 2
    scratch += [dma((chunks,))] * 12
    scratch += [dma((sizes[0] - 1,))] * 2 + [dma((sizes[1] * sizes[2] - 1,))] * 2
    gradient, resid_share, misfit = pl.pallas_call(
        kernel,
        out_shape=[
            jax.ShapeDtypeStruct((cols, rows, depth), f32),
            jax.ShapeDtypeStruct((share, rows, depth), f32),
            jax.ShapeDtypeStruct((1, 1), f32),
        ],
        in_specs=[SMEM, VMEM, VMEM, VMEM, VMEM],
        out_specs=[VMEM, VMEM, SMEM],
        scratch_shapes=scratch,
        compiler_params=pltpu.CompilerParams(collective_id=0, has_side_effects=True),
    )(shifts, w_fwd, w_bwd, volume, measured)
    return (gradient, resid_share, misfit[0, 0])


def solution(mesh):
    in_specs = (P("gx", "gy", "gz"), P(None, None, "gx"), P(None, "gx"), P("gx", "gy", "gz"))
    out_specs = (P("gx", "gy", "gz"), P("gx", "gy", "gz"), P())
    return jax.shard_map(body, mesh=mesh, in_specs=in_specs, out_specs=out_specs, check_vma=False)
```

time: 87.2 us -> 76.3 us (0.87)
  Pallas kernels: 77.6 us -> 68.1 us
  other arithmetic: 1.28 us -> 0 us
    pallas_call x1, Pallas kernels: 77.6 us -> 68.1 us  [body(): pl.pallas_call(kernel, out_shape=[jax.ShapeDtypeStruct((cols, rows, depth...]
    reduce_sum x1 -> x0, other arithmetic: 1.28 us -> none  [body(): misfit = jnp.sum(tile) / entries]
where the time goes in v3:
time: 76.3 us; the launch traced here: 76 us
  Pallas kernels  68.1 us (89%)
  local copies, waits for them, and re-layouts  5.51 us (7%)
  between operations  2.43 us (3%)
    pallas_call x1, Pallas kernels, body(): pl.pallas_call(kernel, out_shape=[jax.ShapeDtypeStruct((cols, rows, depth...  68.1 us
    unnamed x8, local copies, waits for them, and re-layouts  3.83 us

profile of v3, /device:TPU:0, one launch (start us, length us, event | category | flops | bytes accessed | tf_op | source)
XLA Modules:
  0.0 76.0 jit_solution(4259616212615660760)
XLA Ops:
  0.6 0.9 %copy.12 = f32[64,16,8]{0,2,1:T(8,128)S(1)} copy(f32[64,16,8]{0,1,2:T(8,128)} %bitcast.7) | data formatting | bytes 65536
  1.5 0.0 copy-start.1
  1.5 0.7 copy.11.wf_ref
  2.2 0.1 copy-done.1
  2.4 0.2 copy.13
  2.6 0.1 pad.9.clone
  2.6 0.9 %reshape.13.wb_ref = f32[16,1024]{1,0:T(8,128)} reshape(f32[16,64,16]{2,1,0:T(8,128)S(1)} %pad.9.clone) | data formatting | bytes 131072 | tf_op jit(solution)/shard_map/reshape | solution.py:367
  3.5 68.1 %shard_map.67 = (f32[16,64,128]{2,1,0:T(8,128)}, f32[8,64,128]{2,1,0:T(8,128)}, f32[1,1]{1,0:T(1,128)}) custom-call(s32[64]{0:T(128)} %bitcast.8, f32[64,256]{1,0:T(8,128)} %copy.11.wf_ref, f32[16,1024]{1,0:T(8,128)} %reshape.13.wb_ref, f32[16,64,128]{2,1,0:T(8,128)} %vol_ref.1, f32[8,64,128]{2,1,0:T(8,128)} %meas_ref.1), custom_call_target="tpu_custom_call" | custom-call | tf_op jit(solution)/shard_map/pallas_call | solution.py:392
  71.6 0.0 copy-start
  71.6 1.9 %copy.17 = f32[16,64,128]{2,1,0:T(8,128)} copy(f32[16,64,128]{2,1,0:T(8,128)} %get-tuple-element.12) | data formatting | bytes 1048576
  73.6 0.0 copy-done
  73.6 0.7 copy.18
  (2 shorter events, 0.0 us)
Async XLA Ops:
  1.5 0.8 %copy-start.1 = (f32[64,8,16]{0,2,1:T(8,128)S(1)}, f32[64,8,16]{0,2,1:T(8,128)}, u32[]{:S(2)}) copy-start(f32[64,8,16]{0,2,1:T(8,128)} %param.5) | copy-start | bytes 98308
  71.6 1.9 %copy-start = (f32[8,64,128]{2,1,0:T(8,128)S(1)}, f32[8,64,128]{2,1,0:T(8,128)}, u32[]{:S(2)}) copy-start(f32[8,64,128]{2,1,0:T(8,128)} %get-tuple-element.13) | copy-start | bytes 786436

commit v4 on v3

--- a/solution.py
+++ b/solution.py
@@ -10,8 +10,8 @@
 SUB = 8
 WIN = 16
 CHUNK = 2
-SKEW = 2
-LAG = 2
+SKEW = 3
+LAG = 3
 PIECE = 2
 GROUP = 16
 MESH = pl.DeviceIdType.MESH

time: 76.3 us -> 73.3 us (0.961)
  Pallas kernels: 68.1 us -> 65.1 us
    pallas_call x1, Pallas kernels: 68.1 us -> 65.1 us  [body(): pl.pallas_call(kernel, out_shape=[jax.ShapeDtypeStruct((cols, rows, depth...]
where the time goes in v4:
time: 73.3 us; the launch traced here: 73 us
  Pallas kernels  65.1 us (89%)
  local copies, waits for them, and re-layouts  5.51 us (8%)
  between operations  2.43 us (3%)
    pallas_call x1, Pallas kernels, body(): pl.pallas_call(kernel, out_shape=[jax.ShapeDtypeStruct((cols, rows, depth...  65.1 us
    unnamed x8, local copies, waits for them, and re-layouts  3.83 us

profile of v4, /device:TPU:0, one launch (start us, length us, event | category | flops | bytes accessed | tf_op | source)
XLA Modules:
  0.0 73.0 jit_solution(1167992345911427699)
XLA Ops:
  0.6 0.9 %copy.12 = f32[64,16,8]{0,2,1:T(8,128)S(1)} copy(f32[64,16,8]{0,1,2:T(8,128)} %bitcast.7) | data formatting | bytes 65536
  1.5 0.0 copy-start.1
  1.5 0.7 copy.11.wf_ref
  2.2 0.1 copy-done.1
  2.4 0.2 copy.13
  2.6 0.1 pad.9.clone
  2.6 0.9 %reshape.13.wb_ref = f32[16,1024]{1,0:T(8,128)} reshape(f32[16,64,16]{2,1,0:T(8,128)S(1)} %pad.9.clone) | data formatting | bytes 131072 | tf_op jit(solution)/shard_map/reshape | solution.py:367
  3.5 65.1 %shard_map.67 = (f32[16,64,128]{2,1,0:T(8,128)}, f32[8,64,128]{2,1,0:T(8,128)}, f32[1,1]{1,0:T(1,128)}) custom-call(s32[64]{0:T(128)} %bitcast.8, f32[64,256]{1,0:T(8,128)} %copy.11.wf_ref, f32[16,1024]{1,0:T(8,128)} %reshape.13.wb_ref, f32[16,64,128]{2,1,0:T(8,128)} %vol_ref.1, f32[8,64,128]{2,1,0:T(8,128)} %meas_ref.1), custom_call_target="tpu_custom_call" | custom-call | tf_op jit(solution)/shard_map/pallas_call | solution.py:392
  68.6 0.0 copy-start
  68.6 1.9 %copy.17 = f32[16,64,128]{2,1,0:T(8,128)} copy(f32[16,64,128]{2,1,0:T(8,128)} %get-tuple-element.12) | data formatting | bytes 1048576
  70.5 0.0 copy-done
  70.5 0.7 copy.18
  (2 shorter events, 0.0 us)
Async XLA Ops:
  1.5 0.8 %copy-start.1 = (f32[64,8,16]{0,2,1:T(8,128)S(1)}, f32[64,8,16]{0,2,1:T(8,128)}, u32[]{:S(2)}) copy-start(f32[64,8,16]{0,2,1:T(8,128)} %param.5) | copy-start | bytes 98308
  68.6 1.9 %copy-start = (f32[8,64,128]{2,1,0:T(8,128)S(1)}, f32[8,64,128]{2,1,0:T(8,128)}, u32[]{:S(2)}) copy-start(f32[8,64,128]{2,1,0:T(8,128)} %get-tuple-element.13) | copy-start | bytes 786436
